TPU v7x, 32 devices: a whole 2x2x4 slice. The times are simulated.
32 devices in a mesh: qrow: 8 (over y, x, core), kcol: 4 (over z).
Axes of the slice: x: 2, y: 2, z: 4, core: 2. Of those that a mesh axis runs over, the one named last changes fastest.
Arguments:
- query_states: bfloat16 [32768, 512], P(('qrow', 'kcol')), may hold values from -8 to 8
- key_states: bfloat16 [32768, 512], P(('kcol', 'qrow')), may hold values from -8 to 8
- value_states: bfloat16 [32768, 512], P(('kcol', 'qrow')), may hold values from -6 to 6
- saved_output: bfloat16 [32768, 512], P(('qrow', 'kcol')), may hold values from -0.59765625 to 0.59765625
- output_grad: bfloat16 [32768, 512], P(('qrow', 'kcol')), may hold values from -6 to 6
- normalizer: float32 [32768, 4], P(('qrow', 'kcol')), as said below
- doc_lengths: int32 [8], replicated, may hold values from 1 to 8192, as said below
Outputs:
- query_grad: bfloat16 [32768, 512], P(('qrow', 'kcol'))
- key_grad: bfloat16 [32768, 512], P(('kcol', 'qrow'))
- value_grad: bfloat16 [32768, 512], P(('kcol', 'qrow'))
Inputs may be any that keep to these rules, and one draw needn't show every extreme that they name: `doc_lengths`: the 8 lengths sum to 32768; exactly one of them equals 8192, every other one is smaller. normalizer[p, h] is the logarithm of the sum of exp(scores[h, p, t]) over the t that allowed admits, computed in float32 from query_states, key_states and doc_lengths.
All inputs are finite; a program needn't handle non-finite values.
Results may differ from a plain program's by a relative error of at most 0.005.
Values may be sent and summed in bfloat16 or wider, within the bound.
A program may use at most 704 MiB of HBM per device.

v0:
```python
import jax
import jax.numpy as jnp
from jax import lax
from jax.sharding import PartitionSpec as P

HEAD_DIM = 128
KV_HEADS = 4
GROUP = 1
TILES = 8


def document_ids(doc_lengths, positions):
    doc_ends = jnp.cumsum(doc_lengths)
    return jnp.sum((positions[:, None] >= doc_ends[None, :]).astype(jnp.int32), axis=1)


def add_tile(running, query_tile, grad_tile, norm_tile, delta_tile, key_tile, value_tile, allowed):
    query_acc, key_acc, value_acc = running
    query_count = query_tile.shape[0]
    key_count = key_tile.shape[0]
    scaling = HEAD_DIM ** (-0.5)
    query_heads = query_tile.reshape(query_count, KV_HEADS, GROUP, HEAD_DIM)
    grad_heads = grad_tile.reshape(query_count, KV_HEADS, GROUP, HEAD_DIM)
    key_heads = key_tile.reshape(key_count, KV_HEADS, HEAD_DIM)
    value_heads = value_tile.reshape(key_count, KV_HEADS, HEAD_DIM)
    norm_heads = norm_tile.reshape(query_count, KV_HEADS, GROUP).transpose(1, 2, 0)[..., None]
    delta_heads = delta_tile.reshape(query_count, KV_HEADS, GROUP).transpose(1, 2, 0)[..., None]
    scores = (
        jnp.einsum("qhgd,khd->hgqk", query_heads, key_heads, preferred_element_type=jnp.float32)
        * scaling
    )
    probability = jnp.where(allowed[None, None], jnp.exp(scores - norm_heads), 0.0)
    prob_grad = jnp.einsum(
        "qhgd,khd->hgqk", grad_heads, value_heads, preferred_element_type=jnp.float32
    )
    score_grad = probability * (prob_grad - delta_heads)
    prob_half = probability.astype(jnp.bfloat16)
    grad_half = score_grad.astype(jnp.bfloat16)
    value_add = jnp.einsum(
        "hgqk,qhgd->khd", prob_half, grad_heads, preferred_element_type=jnp.float32
    )
    key_add = jnp.einsum(
        "hgqk,qhgd->khd", grad_half, query_heads, preferred_element_type=jnp.float32
    )
    query_add = jnp.einsum(
        "hgqk,khd->qhgd", grad_half, key_heads, preferred_element_type=jnp.float32
    )
    return (
        query_acc + query_add.reshape(query_count, KV_HEADS * GROUP * HEAD_DIM),
        key_acc + key_add.reshape(key_count, KV_HEADS * HEAD_DIM),
        value_acc + value_add.reshape(key_count, KV_HEADS * HEAD_DIM),
    )


def run_tile(running, operands):
    return add_tile(running, *operands)


def per_device(
    query_states, key_states, value_states, saved_output, output_grad, normalizer, doc_lengths
):
    row_index = lax.axis_index("qrow")
    col_index = lax.axis_index("kcol")
    head_count = KV_HEADS * GROUP
    scaling = HEAD_DIM ** (-0.5)
    local_rows = query_states.shape[0]
    row_delta = jnp.sum(
        (output_grad.astype(jnp.float32) * saved_output.astype(jnp.float32)).reshape(
            local_rows, head_count, HEAD_DIM
        ),
        axis=2,
    )
    query_block, grad_block = (
        lax.all_gather(query_states, "kcol", axis=0, tiled=True),
        lax.all_gather(output_grad, "kcol", axis=0, tiled=True),
    )
    norm_block, delta_block = (
        lax.all_gather(normalizer, "kcol", axis=0, tiled=True),
        lax.all_gather(row_delta, "kcol", axis=0, tiled=True),
    )
    key_block, value_block = (
        lax.all_gather(key_states, "qrow", axis=0, tiled=True),
        lax.all_gather(value_states, "qrow", axis=0, tiled=True),
    )
    query_len = query_block.shape[0]
    key_len = key_block.shape[0]
    query_iota = jnp.arange(query_len, dtype=jnp.int32)
    key_iota = jnp.arange(key_len, dtype=jnp.int32)
    query_pos = row_index * query_len + query_iota
    key_pos = col_index * key_len + key_iota
    query_doc = document_ids(doc_lengths, query_pos)
    key_doc = document_ids(doc_lengths, key_pos)
    tile_query = query_len // TILES
    tile_key = key_len // TILES
    key_accs = [
        jnp.zeros((tile_key, KV_HEADS * HEAD_DIM), jnp.float32) for key_step in range(TILES)
    ]
    value_accs = [
        jnp.zeros((tile_key, KV_HEADS * HEAD_DIM), jnp.float32) for key_step in range(TILES)
    ]
    query_parts = []
    for query_step in range(TILES):
        query_lo = query_step * tile_query
        query_hi = query_lo + tile_query
        query_acc = jnp.zeros((tile_query, head_count * HEAD_DIM), jnp.float32)
        for key_step in range(TILES):
            key_lo = key_step * tile_key
            key_hi = key_lo + tile_key
            allowed = (key_pos[key_lo:key_hi][None, :] <= query_pos[query_lo:query_hi][:, None]) & (
                key_doc[key_lo:key_hi][None, :] == query_doc[query_lo:query_hi][:, None]
            )
            operands = (
                query_block[query_lo:query_hi],
                grad_block[query_lo:query_hi],
                norm_block[query_lo:query_hi],
                delta_block[query_lo:query_hi],
                key_block[key_lo:key_hi],
                value_block[key_lo:key_hi],
                allowed,
            )
            running = (query_acc, key_accs[key_step], value_accs[key_step])
            running = run_tile(running, operands)
            query_acc, key_accs[key_step], value_accs[key_step] = running
        query_parts.append(query_acc)
    query_total = jnp.concatenate(query_parts, axis=0) * scaling
    key_total = jnp.concatenate(key_accs, axis=0) * scaling
    value_total = jnp.concatenate(value_accs, axis=0)
    query_grad = lax.psum_scatter(query_total, "kcol", scatter_dimension=0, tiled=True)
    key_grad, value_grad = (
        lax.psum_scatter(key_total, "qrow", scatter_dimension=0, tiled=True),
        lax.psum_scatter(value_total, "qrow", scatter_dimension=0, tiled=True),
    )
    return (
        query_grad.astype(jnp.bfloat16),
        key_grad.astype(jnp.bfloat16),
        value_grad.astype(jnp.bfloat16),
    )


def solution(mesh):
    return jax.shard_map(
        per_device,
        mesh=mesh,
        in_specs=(
            P(("qrow", "kcol"), None),
            P(("kcol", "qrow"), None),
            P(("kcol", "qrow"), None),
            P(("qrow", "kcol"), None),
            P(("qrow", "kcol"), None),
            P(("qrow", "kcol"), None),
            P(),
        ),
        out_specs=(P(("qrow", "kcol"), None), P(("kcol", "qrow"), None), P(("kcol", "qrow"), None)),
        check_vma=False,
    )
```

profile of v0, /device:TPU:0, one launch (start us, length us, event | category | flops | bytes accessed | tf_op | source)
XLA Modules:
  0.0 1663.6 jit_solution(7262917538145876708)
XLA Ops:
  20.6 74.0 %all_gather.23 = f32[4096,4]{1,0:T(8,128)S(1)} all-gather(f32[1024,4]{1,0:T(8,128)S(1)} %reduce_sum.29), channel_id=1, replica_groups=mesh['qrow'=8,'kcol'=4] {'kcol'}, dimensions={0}, use_global_device_ids=true | all-gather | bytes 81920 | tf_op jit(solution)/shard_map/all_gather | solution.py:79
  97.1 15.7 all_gather.20
  113.7 5.3 compare_and_fusion
  119.0 5.2 compare_and_fusion.1
  124.1 5.1 compare_and_fusion.2
  129.3 5.1 compare_and_fusion.3
  134.4 5.1 compare_and_fusion.4
  139.4 5.1 compare_and_fusion.5
  144.6 5.2 compare_and_fusion.6
  149.8 5.1 compare_and_fusion.7
  158.9 50.6 %all-gather.11.cloned.1.call-done = bf16[4096,512]{0,1:T(8,128)(2,1)} async-done(((bf16[1024,512]{0,1:T(8,128)(2,1)}), bf16[4096,512]{0,1:T(8,128)(2,1)}) %all-gather.11.cloned.1.call-update) | async-done | bytes 4194320 | tf_op jit(solution)/shard_map/all_gather | solution.py:75
  213.7 51.1 %all-gather.5.cloned.1.call-done = bf16[8192,512]{0,1:T(8,128)(2,1)} async-done(((bf16[1024,512]{0,1:T(8,128)(2,1)}), bf16[8192,512]{0,1:T(8,128)(2,1)}) %all-gather.5.cloned.1.call-update) | async-done | bytes 8388624 | tf_op jit(solution)/shard_map/all_gather | solution.py:82
  264.7 6.2 fusion.849
  272.4 4.9 fusion.910
  289.6 31.1 %all-gather.9.cloned.1.call-done = bf16[8192,512]{0,1:T(8,128)(2,1)} async-done(((bf16[1024,512]{0,1:T(8,128)(2,1)}), bf16[8192,512]{0,1:T(8,128)(2,1)}) %all-gather.9.cloned.1.call-update) | async-done | bytes 8388624 | tf_op jit(solution)/shard_map/all_gather | solution.py:83
  320.8 6.2 fusion.848
  337.9 4.9 fusion.438
  537.7 5.7 fusion.444
  610.7 5.7 fusion.443
  682.4 5.6 fusion.442
  692.4 4.9 fusion.434
  833.2 9.8 add_add_fusion.1
  849.7 8.0 add_add_fusion.9
  860.8 5.3 fusion.975
  866.0 5.3 fusion.974
  887.2 9.9 add_add_fusion
  903.9 7.9 add_add_fusion.8
  914.8 7.5 fusion.389
  922.3 9.9 add_add_fusion.2
  935.1 7.0 fusion.388
  942.1 9.8 add_add_fusion.3
  954.9 7.0 fusion.387
  962.0 9.8 add_add_fusion.4
  974.8 7.0 fusion.440
  984.9 5.4 fusion.441
  1006.4 7.0 fusion.432
  1016.9 5.6 fusion.433
  1038.0 7.0 fusion.424
  1048.4 5.8 fusion.425
  1069.7 7.0 fusion.416
  1080.2 5.6 fusion.417
  1101.2 7.0 fusion.408
  1111.7 5.6 fusion.409
  1132.8 7.0 fusion.400
  1142.8 6.1 fusion.402
  1167.0 7.0 fusion.392
  1177.0 6.1 fusion.394
  1200.9 7.0 fusion.384
  1211.5 5.7 fusion.386
  1244.0 6.7 fusion.328
  1250.7 6.9 fusion.352
  1257.6 8.6 add_add_fusion.5
  1268.5 5.8 fusion.211
  1274.4 5.5 fusion.235
  1286.7 6.9 fusion.307
  1300.2 8.8 add_add_fusion.6
  1310.9 5.8 fusion.214
  1316.8 5.5 fusion.238
  1329.0 6.9 fusion.310
  1342.5 8.7 add_add_fusion.7
  1368.6 5.0 fusion.961
  1373.7 5.0 fusion.960
  1530.0 6.3 broadcast_multiply_fusion
  1541.7 112.0 %reduce-scatter.6.cloned.1.call-done = f32[1024,512]{1,0:T(8,128)} async-done(((f32[8192,512]{1,0:T(8,128)}), f32[1024,512]{1,0:T(8,128)}) %reduce-scatter.6.cloned.1.call-update) | async-done | bytes 2097168 | tf_op jit(solution)/shard_map/reduce_scatter | solution.py:130
  (1280 shorter events, 932.7 us)
Async XLA Ops:
  7.2 8.7 copy-start.212
  7.2 8.7 copy-start.266
  7.2 147.7 %all-gather.7.cloned.1.call-start = ((), (), s32[]{:S(2)}) async-start(), calls=%async_computation.4 | async-start | bytes 5242880 | tf_op jit(solution)/shard_map/all_gather | solution.py:74
  9.7 199.8 %all-gather.11.cloned.1.call-start = ((), (), s32[]{:S(2)}) async-start(), calls=%async_computation.6 | async-start | bytes 5242880 | tf_op jit(solution)/shard_map/all_gather | solution.py:75
  12.0 252.7 %all-gather.5.cloned.1.call-start = ((), (), s32[]{:S(2)}) async-start(), calls=%async_computation.3 | async-start | bytes 9437184 | tf_op jit(solution)/shard_map/all_gather | solution.py:82
  14.4 306.4 %all-gather.9.cloned.1.call-start = ((), (), s32[]{:S(2)}) async-start(), calls=%async_computation.5 | async-start | bytes 9437184 | tf_op jit(solution)/shard_map/all_gather | solution.py:83
  15.8 1520.5 %reduce-scatter.4.cloned.1.call-start = ((), (), s32[]{:S(2)}) async-start(), calls=%async_computation.7 | async-start | bytes 10485760 | tf_op jit(solution)/shard_map/reduce_scatter | solution.py:128
  17.5 79.5 %copy-start.415 = (s32[8]{0:T(128)S(1)}, s32[8]{0:T(128)}, u32[]{:S(2)}) copy-start(s32[8]{0:T(128)} %param.13) | copy-start | bytes 100
  17.5 79.7 %copy-start.379 = (f32[1024,4]{0,1:T(4,128)S(1)}, f32[1024,4]{0,1:T(4,128)}, u32[]{:S(2)}) copy-start(f32[1024,4]{0,1:T(4,128)} %param.12) | copy-start | bytes 49156
  94.9 587.5 %copy-start.413 = (f32[4,512]{1,0:T(4,128)}, f32[4,512]{1,0:T(4,128)S(1)}, u32[]{:S(2)}) copy-start(f32[4,512]{1,0:T(4,128)S(1)} %copy.1673) | copy-start | bytes 24580
  95.0 597.4 %copy-start.411 = (f32[4,512]{1,0:T(4,128)}, f32[4,512]{1,0:T(4,128)S(1)}, u32[]{:S(2)}) copy-start(f32[4,512]{1,0:T(4,128)S(1)} %copy.1632) | copy-start | bytes 24580
  95.1 606.9 %copy-start.409 = (f32[4,512]{1,0:T(4,128)}, f32[4,512]{1,0:T(4,128)S(1)}, u32[]{:S(2)}) copy-start(f32[4,512]{1,0:T(4,128)S(1)} %copy.1591) | copy-start | bytes 24580
  95.3 615.9 %copy-start.407 = (f32[4,512]{1,0:T(4,128)}, f32[4,512]{1,0:T(4,128)S(1)}, u32[]{:S(2)}) copy-start(f32[4,512]{1,0:T(4,128)S(1)} %copy.1550) | copy-start | bytes 24580
  95.4 624.9 %copy-start.405 = (f32[4,512]{1,0:T(4,128)}, f32[4,512]{1,0:T(4,128)S(1)}, u32[]{:S(2)}) copy-start(f32[4,512]{1,0:T(4,128)S(1)} %copy.1509) | copy-start | bytes 24580
  95.5 562.6 %copy-start.403 = (f32[4,512]{1,0:T(4,128)}, f32[4,512]{1,0:T(4,128)S(1)}, u32[]{:S(2)}) copy-start(f32[4,512]{1,0:T(4,128)S(1)} %copy.1468) | copy-start | bytes 24580
  113.7 544.4 %copy-start.382 = (f32[4,512]{1,0:T(4,128)}, f32[4,512]{1,0:T(4,128)S(1)}, u32[]{:S(2)}) copy-start(f32[4,512]{1,0:T(4,128)S(1)} %get-tuple-element.48) | copy-start | bytes 24580
  113.7 568.7 %copy-start.396 = (f32[4,512]{1,0:T(4,128)}, f32[4,512]{1,0:T(4,128)S(1)}, u32[]{:S(2)}) copy-start(f32[4,512]{1,0:T(4,128)S(1)} %get-tuple-element.43) | copy-start | bytes 24580
  113.7 578.7 %copy-start.393 = (f32[4,512]{1,0:T(4,128)}, f32[4,512]{1,0:T(4,128)S(1)}, u32[]{:S(2)}) copy-start(f32[4,512]{1,0:T(4,128)S(1)} %get-tuple-element.44) | copy-start | bytes 24580
  113.7 588.3 %copy-start.390 = (f32[4,512]{1,0:T(4,128)}, f32[4,512]{1,0:T(4,128)S(1)}, u32[]{:S(2)}) copy-start(f32[4,512]{1,0:T(4,128)S(1)} %get-tuple-element.45) | copy-start | bytes 24580
  113.7 597.4 %copy-start.387 = (f32[4,512]{1,0:T(4,128)}, f32[4,512]{1,0:T(4,128)S(1)}, u32[]{:S(2)}) copy-start(f32[4,512]{1,0:T(4,128)S(1)} %get-tuple-element.46) | copy-start | bytes 24580
  113.7 606.6 %copy-start.384 = (f32[4,512]{1,0:T(4,128)}, f32[4,512]{1,0:T(4,128)S(1)}, u32[]{:S(2)}) copy-start(f32[4,512]{1,0:T(4,128)S(1)} %get-tuple-element.47) | copy-start | bytes 24580
  158.9 257.2 %copy-start.53 = (bf16[512,512]{0,1:T(8,128)(2,1)}, bf16[512,512]{0,1:T(8,128)(2,1)S(1)}, u32[]{:S(2)}) copy-start(bf16[512,512]{0,1:T(8,128)(2,1)S(1)} %get-tuple-element.32) | copy-start | bytes 1572868
  158.9 721.0 %copy-start.51 = (bf16[512,512]{0,1:T(8,128)(2,1)}, bf16[512,512]{0,1:T(8,128)(2,1)S(1)}, u32[]{:S(2)}) copy-start(bf16[512,512]{0,1:T(8,128)(2,1)S(1)} %get-tuple-element.33) | copy-start | bytes 1572868
  271.0 180.9 %copy-start.3 = (bf16[1024,512]{0,1:T(8,128)(2,1)}, bf16[1024,512]{0,1:T(8,128)(2,1)S(1)}, u32[]{:S(2)}) copy-start(bf16[1024,512]{0,1:T(8,128)(2,1)S(1)} %get-tuple-element.12) | copy-start | bytes 3145732
  271.0 185.4 %copy-start.1 = (bf16[1024,512]{0,1:T(8,128)(2,1)}, bf16[1024,512]{0,1:T(8,128)(2,1)S(1)}, u32[]{:S(2)}) copy-start(bf16[1024,512]{0,1:T(8,128)(2,1)S(1)} %get-tuple-element.11) | copy-start | bytes 3145732
  272.3 14.1 copy-start.192
  277.4 9.0 copy-start.307
  277.4 9.0 copy-start.377
  320.8 8.9 copy-start.193
  320.8 9.0 copy-start.308
  320.8 9.1 copy-start.378
  326.9 120.2 %copy-start.259 = (bf16[1024,512]{0,1:T(8,128)(2,1)}, bf16[1024,512]{0,1:T(8,128)(2,1)S(1)}, u32[]{:S(2)}) copy-start(bf16[1024,512]{0,1:T(8,128)(2,1)S(1)} %get-tuple-element.3) | copy-start | bytes 3145732
  451.9 9.1 copy-start.5
  451.9 9.1 copy-start.69
  729.5 9.0 copy-start.41
  765.7 9.3 copy-start
  802.1 9.0 copy-start.171
  819.5 8.9 slice-start.4
  860.7 10.6 copy-start.61
  860.7 10.6 copy-start.164
  874.1 8.5 slice-start.2
  903.9 10.8 copy-start.79
  922.3 12.8 copy-start.239
  942.1 12.8 copy-start.238
  962.0 12.9 copy-start.397
  962.0 12.9 copy-start.414
  1140.6 8.4 slice-start.18
  1174.7 8.4 slice-start.14
  1174.7 8.4 copy-start.250
  1174.7 8.4 copy-start.320
  1242.8 296.2 %reduce-scatter.8.cloned.1.call-start = ((), (), s32[]{:S(2)}) async-start(), calls=%async_computation.9 | async-start | bytes 18874368 | tf_op jit(solution)/shard_map/reduce_scatter | solution.py:131
  1257.6 10.9 copy-start.398
  1268.5 11.4 slice-start.24
  1274.4 8.9 slice-start.22
  1283.4 10.2 slice-start.20
  1286.7 10.2 slice-start.16
  1310.9 11.4 slice-start.12
  1316.8 8.9 slice-start.10
  1325.7 10.2 slice-start.8
  1329.0 10.2 slice-start.6
  1353.1 9.6 copy-start.199
  1378.6 8.7 copy-start.56
  1378.6 275.1 %reduce-scatter.6.cloned.1.call-start = ((), (), s32[]{:S(2)}) async-start(), calls=%async_computation.8 | async-start | bytes 18874368 | tf_op jit(solution)/shard_map/reduce_scatter | solution.py:130
  1401.5 9.4 copy-start.115
  (391 other events, 1586.9 us)
Sparse Core Ops, SparseCore 0:
  10.1 117.7 all-gather.6
  130.1 79.2 all-gather.10
  211.9 52.7 all-gather.4
  266.5 54.2 all-gather.8
  1242.9 144.6 reduce-scatter.3
  1391.0 116.7 reduce-scatter.7
  1536.4 117.2 reduce-scatter.5
where the time goes:
time: 1670 us; the launch traced here: 1660 us
  matrix products  1040 us (62%)
  waiting for transfers between devices  245 us (15%)
  local copies, waits for them, and re-layouts  205 us (12%)
  blocking collectives  89.7 us (5%)
  other arithmetic  63 us (4%)
  between operations  19.8 us (1%)
    dot_general x64, matrix products, add_tile(): jnp.einsum('qhgd,khd->hgqk', grad_heads, value_heads, preferred_element_t...  332 us
    dot_general x64, matrix products, add_tile(): jnp.einsum('hgqk,qhgd->khd', prob_half, grad_heads, preferred_element_typ...  289 us
    dot_general x64, matrix products, add_tile(): jnp.einsum('hgqk,qhgd->khd', grad_half, query_heads, preferred_element_ty...  195 us
    dot_general x64, matrix products, add_tile(): jnp.einsum('qhgd,khd->hgqk', query_heads, key_heads, preferred_element_ty...  170 us
    unnamed x921, local copies, waits for them, and re-layouts  113 us
    reduce_scatter x1, waiting for transfers between devices, per_device(): lax.psum_scatter(key_total, 'qrow', scatter_dimension=0, tiled=True)  112 us
    all_gather x1, blocking collectives, per_device(): lax.all_gather(row_delta, 'kcol', axis=0, tiled=True)  74 us
    dot_general x64, matrix products, add_tile(): jnp.einsum('hgqk,khd->qhgd', grad_half, key_heads, preferred_element_type...  53.4 us
  transfers between devices with their start and end apart: 7, of which 4 were waited for; matrix products, arithmetic and copies ran while one was open for 23% of the time, Pallas kernels for 0%

commit v1 on v0

v1 whole, which is shorter than its diff:
```python
import functools
import math

import jax
import jax.numpy as jnp
from jax import lax
from jax.experimental import pallas as pl
from jax.experimental.pallas import tpu as pltpu
from jax.sharding import Mesh, PartitionSpec as P

HEAD_DIM = 128
KV_HEADS = 4
TILE_Q = 512
TILE_K = 256
SCALING = HEAD_DIM ** (-0.5)
LOG2E = math.log2(math.e)

Q_AXES = ("yx", "core", "ko", "head")
K_AXES = ("ko", "head", "yx", "core")


def dot(a, b, dims):
    return lax.dot_general(a, b, (dims, ((), ())), preferred_element_type=jnp.float32)


def attention_kernel(
    piece, groups, docs, ends_ref, where_ref, q_ref, g_ref, nd_ref, k_ref, v_ref,
    dq_ref, dk_ref, dv_ref, dq_acc, dk_acc, dv_acc,
):
    tile_q = nd_ref.shape[2]
    tile_k = dk_acc.shape[0]
    q_tiles = q_ref.shape[0] // tile_q
    k_tiles = k_ref.shape[0] // tile_k
    core = where_ref[0]
    group = where_ref[1]
    run = 2 * piece

    def key_token(i):
        return (i // run) * (groups * run) + group * run + i % run

    def doc_end(position):
        end = jnp.zeros_like(position)
        for d in range(docs - 1, -1, -1):
            end = jnp.where(position < ends_ref[d], ends_ref[d], end)
        return end

    dq_acc[...] = jnp.zeros_like(dq_acc)
    q_local = lax.broadcasted_iota(jnp.int32, (1, tile_q), 1)
    q_base = (q_local // piece) * run + core * piece + q_local % piece

    def key_step(kt, carry):
        k_lo = kt * tile_k
        rows = pl.ds(pl.multiple_of(k_lo, tile_k), tile_k)
        k = k_ref[rows, :]
        v = v_ref[rows, :]
        k_t = k.T
        k_pos = key_token(k_lo + lax.broadcasted_iota(jnp.int32, (tile_k, 1), 0))
        k_end = doc_end(k_pos)
        first = key_token(k_lo) // (2 * tile_q)
        last = (doc_end(key_token(k_lo + tile_k - 1)) - 1) // (2 * tile_q)
        dk_acc[...] = jnp.zeros_like(dk_acc)
        dv_acc[...] = jnp.zeros_like(dv_acc)

        def query_step(qt, carry):
            q_rows = pl.ds(pl.multiple_of(qt * tile_q, tile_q), tile_q)
            q = q_ref[q_rows, :]
            g = g_ref[q_rows, :]
            nd = nd_ref[qt]
            norm = nd[0:1, :]
            delta = nd[1:2, :]
            q_pos = q_base + qt * (2 * tile_q)
            s = dot(k, q, ((1,), (1,)))
            dp = dot(v, g, ((1,), (1,)))
            allowed = (k_pos <= q_pos) & (q_pos < k_end)
            p = jnp.where(allowed, jnp.exp2(s * (SCALING * LOG2E) - norm), 0.0)
            ds = (p * (dp - delta)).astype(jnp.bfloat16)
            dv_acc[...] += dot(p.astype(jnp.bfloat16), g, ((1,), (0,)))
            dk_acc[...] += dot(ds, q, ((1,), (0,)))
            dq_acc[qt] += dot(k_t, ds, ((1,), (0,)))
            return carry

        lax.fori_loop(first, last + 1, query_step, 0)
        dk_ref[rows, :] = (dk_acc[...] * SCALING).astype(jnp.bfloat16)
        dv_ref[rows, :] = dv_acc[...].astype(jnp.bfloat16)
        return carry

    lax.fori_loop(0, k_tiles, key_step, 0)

    def finish(qt, carry):
        q_rows = pl.ds(pl.multiple_of(qt * tile_q, tile_q), tile_q)
        dq_ref[q_rows, :] = (dq_acc[qt] * SCALING).T.astype(jnp.bfloat16)
        return carry

    lax.fori_loop(0, q_tiles, finish, 0)


def local_attention(piece, groups, ends, place, q, g, nd, k, v):
    tile_q = nd.shape[2]
    tile_k = min(TILE_K, k.shape[0])
    whole = pl.BlockSpec(memory_space=pltpu.VMEM)
    scalars = pl.BlockSpec(memory_space=pltpu.SMEM)
    return pl.pallas_call(
        functools.partial(attention_kernel, piece, groups, ends.shape[0]),
        out_shape=(
            jax.ShapeDtypeStruct(q.shape, jnp.bfloat16),
            jax.ShapeDtypeStruct(k.shape, jnp.bfloat16),
            jax.ShapeDtypeStruct(v.shape, jnp.bfloat16),
        ),
        in_specs=[scalars, scalars, whole, whole, whole, whole, whole],
        out_specs=(whole, whole, whole),
        scratch_shapes=[
            pltpu.VMEM((q.shape[0] // tile_q, HEAD_DIM, tile_q), jnp.float32),
            pltpu.VMEM((tile_k, HEAD_DIM), jnp.float32),
            pltpu.VMEM((tile_k, HEAD_DIM), jnp.float32),
        ],
        compiler_params=pltpu.CompilerParams(vmem_limit_bytes=58 * 1024 * 1024),
    )(ends, place, q, g, nd, k, v)


def per_device(sizes, query_states, key_states, value_states, saved_output, output_grad,
               normalizer, doc_lengths):
    yx, core, ko, head = (sizes[a] for a in Q_AXES)
    devices = yx * core * ko * head
    rows = query_states.shape[0]
    piece = rows // (yx * ko * core)
    groups = yx * ko
    row_delta = jnp.sum(
        (output_grad.astype(jnp.float32) * saved_output.astype(jnp.float32)).reshape(
            rows, KV_HEADS, HEAD_DIM
        ),
        axis=2,
    )

    def deal(x, key_side):
        x = x.reshape(yx, ko, core, piece, KV_HEADS, -1)
        order = (1, 4, 0, 2, 3, 5) if key_side else (0, 2, 1, 4, 3, 5)
        x = x.transpose(order).reshape(devices, piece, x.shape[-1])
        return lax.all_to_all(x, K_AXES if key_side else Q_AXES, 0, 0, tiled=True)

    def undeal(x, key_side):
        x = lax.all_to_all(x, K_AXES if key_side else Q_AXES, 0, 0, tiled=True)
        if key_side:
            x = x.reshape(ko, head, yx, core, piece, HEAD_DIM).transpose(2, 0, 3, 4, 1, 5)
        else:
            x = x.reshape(yx, core, ko, head, piece, HEAD_DIM).transpose(0, 2, 1, 4, 3, 5)
        return x.reshape(rows, KV_HEADS * HEAD_DIM)

    nd = jnp.stack([normalizer * LOG2E, row_delta], axis=-1)
    nd = deal(nd, False)
    q = deal(query_states, False)
    g = deal(output_grad, False)
    k = deal(key_states, True)
    v = deal(value_states, True)

    def gather(x, axes):
        x = lax.all_gather(x, axes, axis=0, tiled=False)
        return x.transpose(1, 0, 2, 3).reshape(-1, x.shape[-1])

    nd = gather(nd, ("yx", "ko"))
    q = gather(q, ("yx", "ko"))
    g = gather(g, ("yx", "ko"))
    k = gather(k, ("core",))
    v = gather(v, ("core",))
    tile_q = min(TILE_Q, q.shape[0])
    nd = nd.reshape(-1, tile_q, 2).transpose(0, 2, 1)
    place = jnp.stack(
        [lax.axis_index("core"), lax.axis_index("yx") * ko + lax.axis_index("ko")]
    ).astype(jnp.int32)
    ends = jnp.cumsum(doc_lengths)
    dq, dk, dv = local_attention(piece, groups, ends, place, q, g, nd, k, v)

    def total(x, parts, axes):
        x = x.reshape(devices, parts, piece, HEAD_DIM).transpose(1, 0, 2, 3)
        x = lax.all_to_all(x, axes, 0, 0, tiled=True)
        return jnp.sum(x.astype(jnp.float32), axis=0).astype(jnp.bfloat16)

    dq = undeal(total(dq, groups, ("yx", "ko")), False)
    dk = undeal(total(dk, core, ("core",)), True)
    dv = undeal(total(dv, core, ("core",)), True)
    return dq, dk, dv


def solution(mesh):
    qrow = mesh.shape["qrow"]
    kcol = mesh.shape["kcol"]
    sizes = {"yx": qrow // 2, "core": 2, "ko": kcol // KV_HEADS, "head": KV_HEADS}
    fine = Mesh(mesh.devices.reshape([sizes[a] for a in Q_AXES]), Q_AXES)
    by_query = P(Q_AXES, None)
    by_key = P(K_AXES, None)
    return jax.shard_map(
        functools.partial(per_device, sizes),
        mesh=fine,
        in_specs=(by_query, by_key, by_key, by_query, by_query, by_query, P()),
        out_specs=(by_query, by_key, by_key),
        check_vma=False,
    )
```

time: 1670 us -> 473 us (0.28)
  matrix products: 1040 us -> 0 us
  local copies, waits for them, and re-layouts: 205 us -> 40.5 us
  waiting for transfers between devices: 245 us -> 165 us
  Pallas kernels: 0 us -> 72.2 us
  other arithmetic: 63 us -> 13.4 us
  blocking collectives: 89.7 us -> 130 us
  starting transfers between devices: 0.29 us -> 36.8 us
    dot_general x320 -> x0, matrix products: 1040 us -> none  [the longest x64 332 us: add_tile(): jnp.einsum('qhgd,khd->hgqk', grad_heads, value_heads, preferred_element_t...]
    all_to_all x0 -> x4, blocking collectives: none -> 121 us  [deal(): return lax.all_to_all(x, K_AXES if key_side else Q_AXES, 0, 0, tiled=True)]
    all_to_all x0 -> x7, waiting for transfers between devices: none -> 117 us  [the longest x3 64.8 us: undeal(): x = lax.all_to_all(x, K_AXES if key_side else Q_AXES, 0, 0, tiled=True)]
    reduce_scatter x3 -> x0, waiting for transfers between devices: 112 us -> none  [the longest x1 112 us: per_device(): lax.psum_scatter(key_total, 'qrow', scatter_dimension=0, tiled=True)]
    unnamed x921 -> x15, local copies, waits for them, and re-layouts: 113 us -> 2.54 us
    all_gather x4, waiting for transfers between devices: 133 us -> 47.9 us  [gather(): x = lax.all_gather(x, axes, axis=0, tiled=False)]
    all_gather x2 -> x1, blocking collectives: 89.7 us -> 8.85 us  [gather(): x = lax.all_gather(x, axes, axis=0, tiled=False)]
    pallas_call x0 -> x1, Pallas kernels: none -> 72.2 us  [local_attention(): pl.pallas_call(functools.partial(attention_kernel, piece, groups, ends.sh...]
  transfers between devices with their start and end apart: 7 -> 11, of which waited for: 4 -> 6; matrix products, arithmetic and copies ran while one was open for 23% -> 9% of each run, Pallas kernels for 0% -> 0%
where the time goes in v1:
time: 473 us; the launch traced here: 471 us
  waiting for transfers between devices  165 us (35%)
  blocking collectives  130 us (27%)
  Pallas kernels  72.2 us (15%)
  local copies, waits for them, and re-layouts  40.5 us (9%)
  starting transfers between devices  36.8 us (8%)
  between operations  14 us (3%)
  other arithmetic  13.4 us (3%)
    all_to_all x4, blocking collectives, deal(): return lax.all_to_all(x, K_AXES if key_side else Q_AXES, 0, 0, tiled=True)  121 us
    pallas_call x1, Pallas kernels, local_attention(): pl.pallas_call(functools.partial(attention_kernel, piece, groups, ends.sh...  72.2 us
    all_to_all x3, waiting for transfers between devices, undeal(): x = lax.all_to_all(x, K_AXES if key_side else Q_AXES, 0, 0, tiled=True)  64.8 us
    all_gather x4, waiting for transfers between devices, gather(): x = lax.all_gather(x, axes, axis=0, tiled=False)  47.9 us
    all_to_all x3, waiting for transfers between devices, total(): x = lax.all_to_all(x, axes, 0, 0, tiled=True)  45.8 us
    all_to_all x3, starting transfers between devices, undeal(): x = lax.all_to_all(x, K_AXES if key_side else Q_AXES, 0, 0, tiled=True)  19.6 us
    transpose x5, local copies, waits for them, and re-layouts, gather(): return x.transpose(1, 0, 2, 3).reshape(-1, x.shape[-1])  15.9 us
    all_to_all x3, starting transfers between devices, total(): x = lax.all_to_all(x, axes, 0, 0, tiled=True)  12.4 us
  transfers between devices with their start and end apart: 11, of which 6 were waited for; matrix products, arithmetic and copies ran while one was open for 9% of the time, Pallas kernels for 0%

profile of v1, /device:TPU:0, one launch (start us, length us, event | category | flops | bytes accessed | tf_op | source)
XLA Modules:
  0.0 471.4 jit_solution(4373128552337968715)
XLA Ops:
  7.2 0.0 all-gather.14.cloned.1.call-start
  7.2 1.3 reshape.116
  8.6 0.2 copy.38
  8.8 0.0 copy-start.2
  8.8 33.4 %all_to_all.55 = bf16[32,128,128]{2,1,0:T(8,128)(2,1)} all-to-all(bf16[32,128,128]{2,1,0:T(8,128)(2,1)S(1)} %bitcast.89), channel_id=1, replica_groups=mesh['yx'=4,'core'=2,'ko'=1,'head'=4] {'ko','head','yx','core'}, dimensions={0} | all-to-all | bytes 2097152 | tf_op jit(solution)/shard_map/all_to_all | solution.py:138
  42.3 0.0 all-gather.14.cloned.1.call-update
  42.3 0.0 all-gather.16.cloned.1.call-start
  42.3 0.3 reshape.119
  42.6 0.2 copy.40
  42.9 0.0 copy-start.3
  42.9 29.7 %all_to_all.56 = bf16[32,128,128]{2,1,0:T(8,128)(2,1)} all-to-all(bf16[32,128,128]{2,1,0:T(8,128)(2,1)S(1)} %bitcast.90), channel_id=1, replica_groups=mesh['yx'=4,'core'=2,'ko'=1,'head'=4] {'ko','head','yx','core'}, dimensions={0} | all-to-all | bytes 2097152 | tf_op jit(solution)/shard_map/all_to_all | solution.py:138
  72.6 0.0 all-gather.16.cloned.1.call-update
  72.7 0.0 all-gather.10.cloned.1.call-start
  72.7 0.3 reshape.108
  73.0 0.2 copy.29
  73.3 28.5 %all_to_all.57 = bf16[32,128,128]{2,1,0:T(8,128)(2,1)} all-to-all(bf16[32,128,128]{2,1,0:T(8,128)(2,1)S(1)} %bitcast.91), channel_id=1, replica_groups=mesh['yx'=4,'core'=2,'ko'=1,'head'=4] {'yx','core','ko','head'}, dimensions={0} | all-to-all | bytes 2097152 | tf_op jit(solution)/shard_map/all_to_all | solution.py:138
  101.7 0.0 all-gather.10.cloned.1.call-update
  101.8 0.0 all-gather.12.cloned.1.call-start
  101.8 0.3 reshape.111
  102.1 0.2 copy.31
  102.4 29.4 %all_to_all.58 = bf16[32,128,128]{2,1,0:T(8,128)(2,1)} all-to-all(bf16[32,128,128]{2,1,0:T(8,128)(2,1)S(1)} %bitcast.92), channel_id=1, replica_groups=mesh['yx'=4,'core'=2,'ko'=1,'head'=4] {'yx','core','ko','head'}, dimensions={0} | all-to-all | bytes 2097152 | tf_op jit(solution)/shard_map/all_to_all | solution.py:138
  131.8 0.0 all-gather.12.cloned.1.call-update
  131.8 1.7 convert_multiply_fusion
  133.5 1.9 reshape.114
  135.4 0.0 copy-start.5
  135.4 0.0 copy-start.6
  135.4 1.2 reduce_sum.45
  136.6 0.2 copy.33
  136.8 0.6 copy.35
  137.5 4.7 all-to-all-start.2
  142.2 0.7 reduce-window.9
  142.8 0.6 pad_add_fusion.where_ref
  143.4 6.0 %all-to-all-done.2 = f32[32,128,2]{1,2,0:T(2,128)S(1)} async-done(((f32[32,128,2]{1,2,0:T(2,128)}), f32[32,128,2]{1,2,0:T(2,128)S(1)}, u32[]{:S(2)}, u32[]{:S(2)}) %all-to-all-start.2) | async-done | bytes 32800 | tf_op jit(solution)/shard_map/all_to_all | solution.py:138
  149.4 8.8 %all-gather.2 = f32[128,128,2]{1,0,2:T(8,128)S(1)} all-gather(f32[32,128,2]{1,0,2:T(8,128)S(1)} %copy.36), channel_id=4, replica_groups=mesh['yx'=4,'core'=2,'ko'=1,'head'=4] {'yx','ko'}, dimensions={0}, use_global_device_ids=true | all-gather | bytes 163840 | tf_op jit(solution)/shard_map/all_gather | solution.py:156
  158.3 0.1 copy.37
  158.4 0.8 reshape_reshape.3
  159.1 3.2 copy.39
  162.3 3.1 copy.41
  165.5 4.7 %copy.30 = bf16[32,4,128,128]{3,2,1,0:T(8,128)(2,1)} copy(bf16[32,4,128,128]{3,2,0,1:T(8,128)(2,1)} %bitcast.83) | data formatting | bytes 8388608 | tf_op jit(solution)/shard_map/transpose | solution.py:157
  170.2 47.9 %all-gather.12.cloned.1.call-done = bf16[128,128,128]{2,1,0:T(8,128)(2,1)} async-done(((bf16[32,128,128]{2,1,0:T(8,128)(2,1)}), bf16[128,128,128]{2,1,0:T(8,128)(2,1)}) %all-gather.12.cloned.1.call-update) | async-done | bytes 4194320 | tf_op jit(solution)/shard_map/all_gather | solution.py:156
  218.2 4.8 %copy.32 = bf16[32,4,128,128]{3,2,1,0:T(8,128)(2,1)} copy(bf16[32,4,128,128]{3,2,0,1:T(8,128)(2,1)} %bitcast.84) | data formatting | bytes 8388608 | tf_op jit(solution)/shard_map/transpose | solution.py:157
  222.9 72.2 %shard_map.94 = (bf16[16384,128]{1,0:T(8,128)(2,1)}, bf16[8192,128]{1,0:T(8,128)(2,1)}, bf16[8192,128]{1,0:T(8,128)(2,1)}) custom-call(s32[8]{0:T(128)} %bitcast.110, s32[2]{0:T(128)} %pad_add_fusion.where_ref, bf16[16384,128]{1,0:T(8,128)(2,1)} %bitcast.76, bf16[16384,128]{1,0:T(8,128)(2,1)} %bitcast.77, f32[32,2,512]{2,1,0:T(2,128)} %bitcast.105, ...), custom_call_target="tpu_custom_call" | custom-call | tf_op jit(solution)/shard_map/pallas_call | solution.py:102
  295.2 3.2 copy.59
  298.4 3.8 all-to-all-start.7
  302.1 3.2 copy.58
  305.3 1.4 copy-done
  306.7 3.8 all-to-all-start.9
  310.5 3.3 reduce_sum.47
  313.8 12.6 %all-to-all-start.8 = ((bf16[32,128,128]{2,1,0:T(8,128)(2,1)}), bf16[32,128,128]{2,1,0:T(8,128)(2,1)S(1)}, u32[]{:S(2)}, u32[]{:S(2)}) async-start(bf16[32,128,128]{2,1,0:T(8,128)(2,1)} %reduce_sum.47), calls=%async_computation.8 | async-start | bytes 2097152 | tf_op jit(solution)/shard_map/all_to_all | solution.py:141
  326.4 4.8 %copy.57 = bf16[32,4,128,128]{3,2,0,1:T(8,128)(2,1)} copy(bf16[32,4,128,128]{3,2,1,0:T(8,128)(2,1)} %bitcast.85) | data formatting | bytes 8388608 | tf_op jit(solution)/shard_map/reshape | solution.py:173
  331.2 21.4 %all-to-all-done.8 = bf16[32,128,128]{2,1,0:T(8,128)(2,1)S(1)} async-done(((bf16[32,128,128]{2,1,0:T(8,128)(2,1)}), bf16[32,128,128]{2,1,0:T(8,128)(2,1)S(1)}, u32[]{:S(2)}, u32[]{:S(2)}) %all-to-all-start.8) | async-done | bytes 1048608 | tf_op jit(solution)/shard_map/all_to_all | solution.py:141
  352.6 4.9 %all-to-all-start.5 = ((bf16[4,32,128,128]{3,2,1,0:T(8,128)(2,1)}), bf16[4,32,128,128]{3,2,1,0:T(8,128)(2,1)}, u32[]{:S(2)}, u32[]{:S(2)}) async-start(bf16[4,32,128,128]{3,2,1,0:T(8,128)(2,1)} %bitcast.78), calls=%async_computation.5 | async-start | bytes 8388608 | tf_op jit(solution)/shard_map/all_to_all | solution.py:174
  357.5 1.7 reduce_sum.48
  359.2 45.8 %all-to-all-done.5 = bf16[4,32,128,128]{3,2,1,0:T(8,128)(2,1)} async-done(((bf16[4,32,128,128]{3,2,1,0:T(8,128)(2,1)}), bf16[4,32,128,128]{3,2,1,0:T(8,128)(2,1)}, u32[]{:S(2)}, u32[]{:S(2)}) %all-to-all-start.5) | async-done | bytes 4194336 | tf_op jit(solution)/shard_map/all_to_all | solution.py:174
  405.0 3.2 all-to-all-start.10
  408.1 4.3 reduce_sum.46
  412.4 22.0 %all-to-all-done.10 = bf16[32,128,128]{2,1,0:T(8,128)(2,1)S(1)} async-done(((bf16[32,128,128]{2,1,0:T(8,128)(2,1)}), bf16[32,128,128]{2,1,0:T(8,128)(2,1)S(1)}, u32[]{:S(2)}, u32[]{:S(2)}) %all-to-all-start.10) | async-done | bytes 1048608 | tf_op jit(solution)/shard_map/all_to_all | solution.py:141
  434.3 3.8 all-to-all-start.6
  438.2 0.8 copy.45
  439.0 0.8 copy.47
  439.8 1.7 copy_bitcast_fusion.3
  441.5 21.4 %all-to-all-done.6 = bf16[32,128,128]{2,1,0:T(8,128)(2,1)S(1)} async-done(((bf16[32,128,128]{2,1,0:T(8,128)(2,1)}), bf16[32,128,128]{2,1,0:T(8,128)(2,1)S(1)}, u32[]{:S(2)}, u32[]{:S(2)}) %all-to-all-start.6) | async-done | bytes 1048608 | tf_op jit(solution)/shard_map/all_to_all | solution.py:141
  462.9 0.8 copy.43
  463.7 1.2 copy.60
  (18 shorter events, 0.1 us)
Async XLA Ops:
  7.2 152.0 %all-gather.14.cloned.1.call-start = ((), (), s32[]{:S(2)}) async-start(), calls=%async_computation.13 | async-start | bytes 3145728 | tf_op jit(solution)/shard_map/all_gather | solution.py:156
  8.8 33.5 %copy-start.2 = (bf16[1024,512]{1,0:T(8,128)(2,1)S(1)}, bf16[1024,512]{1,0:T(8,128)(2,1)}, u32[]{:S(2)}) copy-start(bf16[1024,512]{1,0:T(8,128)(2,1)} %param.9) | copy-start | bytes 3145732
  42.3 120.0 %all-gather.16.cloned.1.call-start = ((), (), s32[]{:S(2)}) async-start(), calls=%async_computation.14 | async-start | bytes 3145728 | tf_op jit(solution)/shard_map/all_gather | solution.py:156
  42.9 29.8 %copy-start.3 = (bf16[1024,512]{1,0:T(8,128)(2,1)S(1)}, bf16[1024,512]{1,0:T(8,128)(2,1)}, u32[]{:S(2)}) copy-start(bf16[1024,512]{1,0:T(8,128)(2,1)} %param.7) | copy-start | bytes 3145732
  72.7 92.8 %all-gather.10.cloned.1.call-start = ((), (), s32[]{:S(2)}) async-start(), calls=%async_computation.11 | async-start | bytes 5242880 | tf_op jit(solution)/shard_map/all_gather | solution.py:156
  73.3 28.5 %copy-start.1 = (bf16[1024,512]{1,0:T(8,128)(2,1)S(1)}, bf16[1024,512]{1,0:T(8,128)(2,1)}, u32[]{:S(2)}) copy-start(bf16[1024,512]{1,0:T(8,128)(2,1)} %param.11) | copy-start | bytes 3145732
  101.8 116.4 %all-gather.12.cloned.1.call-start = ((), (), s32[]{:S(2)}) async-start(), calls=%async_computation.12 | async-start | bytes 5242880 | tf_op jit(solution)/shard_map/all_gather | solution.py:156
  102.4 29.4 %copy-start.4 = (bf16[1024,512]{1,0:T(8,128)(2,1)S(1)}, bf16[1024,512]{1,0:T(8,128)(2,1)}, u32[]{:S(2)}) copy-start(bf16[1024,512]{1,0:T(8,128)(2,1)} %param.10) | copy-start | bytes 3145732
  135.4 1.4 copy-start.5
  135.4 6.7 %copy-start.6 = (s32[8]{0:T(128)S(1)}, s32[8]{0:T(128)}, u32[]{:S(2)}) copy-start(s32[8]{0:T(128)} %param.13) | copy-start | bytes 100
  137.5 12.0 %all-to-all-start.2 = ((f32[32,128,2]{1,2,0:T(2,128)}), f32[32,128,2]{1,2,0:T(2,128)S(1)}, u32[]{:S(2)}, u32[]{:S(2)}) async-start(f32[32,128,2]{1,2,0:T(2,128)} %copy.35), calls=%async_computation.2 | async-start | bytes 65536 | tf_op jit(solution)/shard_map/all_to_all | solution.py:138
  298.4 7.0 %all-to-all-start.7 = ((bf16[2,32,128,128]{3,2,1,0:T(8,128)(2,1)}), bf16[2,32,128,128]{3,2,1,0:T(8,128)(2,1)S(1)}, u32[]{:S(2)}, u32[]{:S(2)}) async-start(bf16[2,32,128,128]{3,2,1,0:T(8,128)(2,1)} %bitcast.82), calls=%async_computation.7 | async-start | bytes 4194304 | tf_op jit(solution)/shard_map/all_to_all | solution.py:174
  305.3 1.4 copy-start
  306.7 7.1 %all-to-all-start.9 = ((bf16[2,32,128,128]{3,2,1,0:T(8,128)(2,1)}), bf16[2,32,128,128]{3,2,1,0:T(8,128)(2,1)S(1)}, u32[]{:S(2)}, u32[]{:S(2)}) async-start(bf16[2,32,128,128]{3,2,1,0:T(8,128)(2,1)} %bitcast.81), calls=%async_computation.9 | async-start | bytes 4194304 | tf_op jit(solution)/shard_map/all_to_all | solution.py:174
  313.8 38.9 %all-to-all-start.8 = ((bf16[32,128,128]{2,1,0:T(8,128)(2,1)}), bf16[32,128,128]{2,1,0:T(8,128)(2,1)S(1)}, u32[]{:S(2)}, u32[]{:S(2)}) async-start(bf16[32,128,128]{2,1,0:T(8,128)(2,1)} %reduce_sum.47), calls=%async_computation.8 | async-start | bytes 2097152 | tf_op jit(solution)/shard_map/all_to_all | solution.py:141
  352.6 52.3 %all-to-all-start.5 = ((bf16[4,32,128,128]{3,2,1,0:T(8,128)(2,1)}), bf16[4,32,128,128]{3,2,1,0:T(8,128)(2,1)}, u32[]{:S(2)}, u32[]{:S(2)}) async-start(bf16[4,32,128,128]{3,2,1,0:T(8,128)(2,1)} %bitcast.78), calls=%async_computation.5 | async-start | bytes 8388608 | tf_op jit(solution)/shard_map/all_to_all | solution.py:174
  405.0 29.4 %all-to-all-start.10 = ((bf16[32,128,128]{2,1,0:T(8,128)(2,1)}), bf16[32,128,128]{2,1,0:T(8,128)(2,1)S(1)}, u32[]{:S(2)}, u32[]{:S(2)}) async-start(bf16[32,128,128]{2,1,0:T(8,128)(2,1)} %reduce_sum.48), calls=%async_computation.10 | async-start | bytes 2097152 | tf_op jit(solution)/shard_map/all_to_all | solution.py:141
  434.3 28.6 %all-to-all-start.6 = ((bf16[32,128,128]{2,1,0:T(8,128)(2,1)}), bf16[32,128,128]{2,1,0:T(8,128)(2,1)S(1)}, u32[]{:S(2)}, u32[]{:S(2)}) async-start(bf16[32,128,128]{2,1,0:T(8,128)(2,1)} %reduce_sum.46), calls=%async_computation.6 | async-start | bytes 2097152 | tf_op jit(solution)/shard_map/all_to_all | solution.py:141
Sparse Core Ops, SparseCore 0:
  42.4 9.5 all-gather.13
  72.8 9.5 all-gather.15
  101.9 61.9 all-gather.9
  165.6 52.5 all-gather.11
